TPU v7x, 32 devices: a 4x2x2 block of a 4x4x8 slice. The times are simulated.
32 devices in a mesh: dp: 4 (over y, z), tp: 8 (over x, core).
Axes of the slice: x: 4, y: 2, z: 2, core: 2. Of those that a mesh axis runs over, the one named last changes fastest.
The devices are a block of a 4x4x8 slice.
Arguments:
- x_steps: bfloat16 [4, 2048, 512], P(None, 'dp'), parts along dimension 1
- conv_state: bfloat16 [2048, 1024, 3], P('dp', 'tp'), parts along dimension 0
- ssm_state: float32 [2048, 1024, 16], P('dp', 'tp'), parts along dimension 0
- expert_ids: int32 [4, 2048, 1], P(None, 'dp'), parts along dimension 1
- g_in: bfloat16 [512], replicated
- w_in: bfloat16 [512, 2, 1024], P(None, None, 'tp')
- conv_w: bfloat16 [1024, 4], P('tp')
- conv_b: bfloat16 [1024], P('tp')
- w_xp: bfloat16 [1024, 64], P('tp')
- g_dt: bfloat16 [32], replicated
- g_b: bfloat16 [16], replicated
- g_c: bfloat16 [16], replicated
- w_dt: bfloat16 [32, 1024], P(None, 'tp')
- b_dt: bfloat16 [1024], P('tp')
- a_log: float32 [1024, 16], P('tp')
- d_skip: float32 [1024], P('tp')
- w_out: bfloat16 [1024, 512], P('tp')
- g_ff: bfloat16 [512], replicated
- w_router: bfloat16 [512, 16], replicated
- w_gate: bfloat16 [16, 512, 2048], P(None, None, 'tp')
- w_up: bfloat16 [16, 512, 2048], P(None, None, 'tp')
- w_down: bfloat16 [16, 2048, 512], P(None, 'tp')
Outputs:
- output 1: bfloat16 [4, 2048, 512], P(None, 'dp'), parts along dimension 1
- output 2: bfloat16 [2048, 1024, 3], P('dp', 'tp'), parts along dimension 0
- output 3: float32 [2048, 1024, 16], P('dp', 'tp'), parts along dimension 0
There are 4 independent parts. A program takes and returns all parts, laid end to end along the dimension named above; an argument that names none is the same for every part.
All inputs are finite; a program needn't handle non-finite values.
Results may differ from a plain program's by a relative error of at most 0.015917.
Values are sent between devices in bfloat16 or wider.
A program may use at most 768 MiB of HBM per device.

v0:
```python
import jax
import jax.numpy as jnp
from jax import lax
from jax.sharding import PartitionSpec as P

EPSILON = 1e-6


def rms_norm(tensor_in, gain_vec):
    in_f32 = tensor_in.astype(jnp.float32)
    return in_f32 * lax.rsqrt(jnp.mean(in_f32 * in_f32, axis=-1, keepdims=True) + EPSILON) * gain_vec.astype(jnp.float32)


def solution(mesh):
    act_spec = P(None, "dp", None)
    state_spec = P("dp", "tp", None)
    in_specs = (act_spec, state_spec, state_spec, act_spec, P(None), P(None, None, "tp"), P("tp", None), P("tp"), P("tp", None), P(None), P(None), P(None), P(None, "tp"), P("tp"), P("tp", None), P("tp"), P("tp", None), P(None), P(None, None), P(None, None, "tp"), P(None, None, "tp"), P(None, "tp", None))
    out_specs = (act_spec, state_spec, state_spec)

    def layer_steps(x_steps, conv_state, ssm_state, expert_ids, g_in, w_in, conv_w, conv_b, w_xp, g_dt, g_b, g_c, w_dt, b_dt, a_log, d_skip, w_out, g_ff, w_router, w_gate, w_up, w_down):
        num_steps, batch_loc, d_model = x_steps.shape
        inner_loc = w_in.shape[2]
        dt_rank = w_dt.shape[0]
        state_dim = a_log.shape[1]
        experts = w_gate.shape[0]
        top_k = expert_ids.shape[2]
        route_rows = batch_loc * top_k
        w_in_flat = w_in.reshape(d_model, 2 * inner_loc)
        a_mat = -jnp.exp(a_log)
        conv_wf = conv_w.astype(jnp.float32)
        conv_bf = conv_b.astype(jnp.float32)
        dt_bias = b_dt.astype(jnp.float32)
        conv_st = conv_state
        ssm_st = ssm_state
        step_outs = []
        for step_idx in range(num_steps):
            x_now = x_steps[step_idx]
            ids_now = expert_ids[step_idx]
            norm_in = rms_norm(x_now, g_in).astype(jnp.bfloat16)
            proj_xz = jnp.dot(norm_in, w_in_flat, preferred_element_type=jnp.float32).astype(jnp.bfloat16).reshape(batch_loc, 2, inner_loc)
            x_inner = proj_xz[:, 0]
            z_gate = proj_xz[:, 1]
            conv_win = jnp.concatenate([conv_st, x_inner[:, :, None]], axis=2)
            x_conv = jax.nn.silu(jnp.sum(conv_win.astype(jnp.float32) * conv_wf[None], axis=2) + conv_bf[None]).astype(jnp.bfloat16)
            conv_st = conv_win[:, :, 1:]
            proj_sum = lax.psum(jnp.dot(x_conv, w_xp, preferred_element_type=jnp.float32), "tp")
            dt_low = rms_norm(proj_sum[:, :dt_rank], g_dt)
            b_vec = rms_norm(proj_sum[:, dt_rank:dt_rank + state_dim], g_b)
            c_vec = rms_norm(proj_sum[:, dt_rank + state_dim:], g_c)
            delta_t = jax.nn.softplus(jnp.dot(dt_low.astype(jnp.bfloat16), w_dt, preferred_element_type=jnp.float32) + dt_bias[None])
            xc_f32 = x_conv.astype(jnp.float32)
            ssm_st = jnp.exp(delta_t[:, :, None] * a_mat[None]) * ssm_st + (delta_t * xc_f32)[:, :, None] * b_vec[:, None, :]
            y_gated = ((jnp.sum(ssm_st * c_vec[:, None, :], axis=2) + d_skip[None] * xc_f32) * jax.nn.silu(z_gate.astype(jnp.float32))).astype(jnp.bfloat16)
            mix_sum = lax.psum(jnp.dot(y_gated, w_out, preferred_element_type=jnp.float32).astype(jnp.bfloat16), "tp")
            resid_mid = (x_now.astype(jnp.float32) + mix_sum.astype(jnp.float32)).astype(jnp.bfloat16)
            moe_in = rms_norm(resid_mid, g_ff).astype(jnp.bfloat16)
            route_prob = jax.nn.softmax(jnp.dot(moe_in, w_router, preferred_element_type=jnp.float32), axis=-1)
            flat_ids = ids_now.reshape(route_rows)
            sort_order = jnp.argsort(flat_ids, stable=True)
            tok_rows = sort_order // top_k
            counts = jnp.bincount(flat_ids, length=experts).astype(jnp.int32)
            x_rows = jnp.take(moe_in, tok_rows, axis=0)
            gate_h = lax.ragged_dot(x_rows, w_gate, counts, preferred_element_type=jnp.float32)
            up_h = lax.ragged_dot(x_rows, w_up, counts, preferred_element_type=jnp.float32)
            hidden = (jax.nn.silu(gate_h) * up_h).astype(jnp.bfloat16)
            y_rows = lax.ragged_dot(hidden, w_down, counts, preferred_element_type=jnp.float32)
            gate_rows = jnp.take(jnp.take_along_axis(route_prob, ids_now, axis=1).reshape(route_rows), sort_order)
            moe_part = jax.ops.segment_sum(y_rows * gate_rows[:, None], tok_rows, num_segments=batch_loc)
            moe_sum = lax.psum(moe_part.astype(jnp.bfloat16), "tp")
            step_outs.append((resid_mid.astype(jnp.float32) + moe_sum.astype(jnp.float32)).astype(jnp.bfloat16))
        return jnp.stack(step_outs), conv_st, ssm_st

    return jax.shard_map(layer_steps, mesh=mesh, in_specs=in_specs, out_specs=out_specs, check_vma=False)
```

profile of v0, /device:TPU:80, one launch (start us, length us, event | category | flops | bytes accessed | tf_op | source)
XLA Modules:
  0.0 461.1 jit_solution(15182430367833714363)
XLA Ops:
  28.5 3.8 sort.59
  32.2 3.8 sort.60
  36.6 3.8 sort.62
  52.6 31.2 %all-reduce.7.cloned.1.call-done = (f32[512,64]{0,1:T(8,128)}, f32[512,64]{0,1:T(8,128)}, f32[512,64]{0,1:T(8,128)}, f32[512,64]{0,1:T(8,128)}) async-done(((f32[512,64]{0,1:T(8,128)}, f32[512,64]{0,1:T(8,128)}, f32[512,64]{0,1:T(8,128)}, f32[512,64]{0,1:T(8,128)}), (f32[512,64]{0,1:T(8,128)}, f32[512,64]{0,1:T(8,128)}, f32[512,64]{0,1:T(8,128)}, f32[512,64]{0,1:T(8,128)})) %all-reduce.7.cloned.1.call-update) | async-done | bytes 524304 | tf_op jit(solution)/shard_map/psum | solution.py:46
  107.7 13.4 %multiply_reduce_fusion = (f32[512,128]{1,0:T(8,128)S(1)}, f32[512,128,16]{1,2,0:T(8,128)}, f32[512,128]{1,0:T(8,128)S(1)}, f32[512,128]{1,0:T(8,128)S(1)}, f32[512,128]{1,0:T(8,128)S(1)}) fusion(f32[512,16]{1,0:T(8,128)} %copy.49, f32[512,16]{1,0:T(8,128)} %copy.48, f32[512,128]{1,0:T(8,128)S(1)} %get-tuple-element.164, f32[512,16]{1,0:T(8,128)} %copy.44, ...), kind=kLoop, calls=%fused_computation.20 | loop fusion | flops 24903680 | bytes 11804672 | tf_op jit(solution)/shard_map/reduce_sum | solution.py:53
  125.9 4.8 %scatter_custom_fusion = s32[16]{0:T(128)} fusion(s32[512]{0:T(512)} %bitcast.242, s32[512]{0:T(512)S(1)} %broadcast.454, s32[]{:T(128)} %constant.124.clone.1), kind=kCustom, calls=%fused_computation.363 | custom fusion | flops 512 | bytes 576 | tf_op jit(solution)/shard_map/scatter-add | solution.py:61
  130.7 4.8 %scatter_custom_fusion.2 = s32[16]{0:T(128)} fusion(s32[512]{0:T(512)} %bitcast.241, s32[512]{0:T(512)S(1)} %broadcast.454, s32[]{:T(128)} %constant.124.clone.1), kind=kCustom, calls=%fused_computation.361 | custom fusion | flops 512 | bytes 576 | tf_op jit(solution)/shard_map/scatter-add | solution.py:61
  135.5 4.8 %scatter_custom_fusion.4 = s32[16]{0:T(128)} fusion(s32[512]{0:T(512)} %bitcast.240, s32[512]{0:T(512)S(1)} %broadcast.454, s32[]{:T(128)} %constant.124.clone.1), kind=kCustom, calls=%fused_computation.359 | custom fusion | flops 512 | bytes 576 | tf_op jit(solution)/shard_map/scatter-add | solution.py:61
  140.3 4.7 %scatter_custom_fusion.6 = s32[16]{0:T(128)} fusion(s32[512]{0:T(512)} %bitcast.239, s32[512]{0:T(512)S(1)} %broadcast.454, s32[]{:T(128)} %constant.124.clone.1), kind=kCustom, calls=%fused_computation.357 | custom fusion | flops 512 | bytes 576 | tf_op jit(solution)/shard_map/scatter-add | solution.py:61
  152.2 3.8 sort.61
  156.1 28.5 %all-reduce.11.cloned.1.call-done = (bf16[512,512]{1,0:T(8,128)(2,1)}, bf16[512,512]{1,0:T(8,128)(2,1)}, bf16[512,512]{1,0:T(8,128)(2,1)}, bf16[512,512]{1,0:T(8,128)(2,1)}) async-done(((bf16[512,512]{1,0:T(8,128)(2,1)}, bf16[512,512]{1,0:T(8,128)(2,1)}, bf16[512,512]{1,0:T(8,128)(2,1)}, bf16[512,512]{1,0:T(8,128)(2,1)}), (bf16[512,512]{1,0:T(8,128)(2,1)}, bf16[512,512]{1,0:T(8,128)(2,1)}, ...) | async-done | bytes 2097168 | tf_op jit(solution)/shard_map/psum | solution.py:54
  194.1 4.5 gather_fusion.1
  198.6 4.5 gather_fusion.4
  203.2 4.5 gather_fusion.7
  207.8 4.5 gather_fusion.10
  220.3 8.7 %ragged-dot-none.1 = f32[512,256]{1,0:T(8,128)} custom-call(s32[1]{0:T(128)} %get-tuple-element.14, s32[17]{0:T(128)} %get-tuple-element.15, s32[17]{0:T(128)} %get-tuple-element.16, s32[17]{0:T(128)} %get-tuple-element.17, s32[1]{0:T(128)} %get-tuple-element.14, bf16[512,512]{1,0:T(8,128)(2,1)} %broadcast_select_fusion, bf16[16,512,256]{2,1,0:T(8,128)(2,1)} %param.48), custom_call_target="tpu_custom_call" | custom-call | flops 134217728 | bytes 5242944 | tf_op jit(solution)/shard_map/ragged_dot_general/ragged-dot-none
  229.1 8.7 %ragged-dot-none.2 = f32[512,256]{1,0:T(8,128)} custom-call(s32[1]{0:T(128)} %get-tuple-element.14, s32[17]{0:T(128)} %get-tuple-element.15, s32[17]{0:T(128)} %get-tuple-element.16, s32[17]{0:T(128)} %get-tuple-element.17, s32[1]{0:T(128)} %get-tuple-element.14, bf16[512,512]{1,0:T(8,128)(2,1)} %broadcast_select_fusion, bf16[16,512,256]{2,1,0:T(8,128)(2,1)} %param.47), custom_call_target="tpu_custom_call" | custom-call | flops 134217728 | bytes 5242944 | tf_op jit(solution)/shard_map/ragged_dot_general/ragged-dot-none
  238.7 10.0 %ragged-dot-none.4 = f32[512,256]{1,0:T(8,128)} custom-call(s32[1]{0:T(128)} %get-tuple-element.26, s32[17]{0:T(128)} %get-tuple-element.27, s32[17]{0:T(128)} %get-tuple-element.28, s32[17]{0:T(128)} %get-tuple-element.29, s32[1]{0:T(128)} %get-tuple-element.26, bf16[512,512]{1,0:T(8,128)(2,1)} %broadcast_select_fusion.1, bf16[16,512,256]{2,1,0:T(8,128)(2,1)} %param.48), custom_call_target="tpu_custom_call" | custom-call | flops 134217728 | bytes 5242944 | tf_op jit(solution)/shard_map/ragged_dot_general/ragged-dot-none
  248.7 10.0 %ragged-dot-none.5 = f32[512,256]{1,0:T(8,128)} custom-call(s32[1]{0:T(128)} %get-tuple-element.26, s32[17]{0:T(128)} %get-tuple-element.27, s32[17]{0:T(128)} %get-tuple-element.28, s32[17]{0:T(128)} %get-tuple-element.29, s32[1]{0:T(128)} %get-tuple-element.26, bf16[512,512]{1,0:T(8,128)(2,1)} %broadcast_select_fusion.1, bf16[16,512,256]{2,1,0:T(8,128)(2,1)} %param.47), custom_call_target="tpu_custom_call" | custom-call | flops 134217728 | bytes 5242944 | tf_op jit(solution)/shard_map/ragged_dot_general/ragged-dot-none
  265.1 13.8 %ragged-dot-none.10 = f32[512,256]{1,0:T(8,128)} custom-call(s32[1]{0:T(128)} %get-tuple-element.50, s32[17]{0:T(128)} %get-tuple-element.51, s32[17]{0:T(128)} %get-tuple-element.52, s32[17]{0:T(128)} %get-tuple-element.53, s32[1]{0:T(128)} %get-tuple-element.50, bf16[512,512]{1,0:T(8,128)(2,1)} %broadcast_select_fusion.3, bf16[16,512,256]{2,1,0:T(8,128)(2,1)} %param.48), custom_call_target="tpu_custom_call" | custom-call | flops 134217728 | bytes 5242944 | tf_op jit(solution)/shard_map/ragged_dot_general/ragged-dot-none
  278.8 13.6 %ragged-dot-none.11 = f32[512,256]{1,0:T(8,128)} custom-call(s32[1]{0:T(128)} %get-tuple-element.50, s32[17]{0:T(128)} %get-tuple-element.51, s32[17]{0:T(128)} %get-tuple-element.52, s32[17]{0:T(128)} %get-tuple-element.53, s32[1]{0:T(128)} %get-tuple-element.50, bf16[512,512]{1,0:T(8,128)(2,1)} %broadcast_select_fusion.3, bf16[16,512,256]{2,1,0:T(8,128)(2,1)} %param.47), custom_call_target="tpu_custom_call" | custom-call | flops 134217728 | bytes 5242944 | tf_op jit(solution)/shard_map/ragged_dot_general/ragged-dot-none
  298.8 9.1 %ragged-dot-none.7 = f32[512,256]{1,0:T(8,128)} custom-call(s32[1]{0:T(128)} %get-tuple-element.38, s32[17]{0:T(128)} %get-tuple-element.39, s32[17]{0:T(128)} %get-tuple-element.40, s32[17]{0:T(128)} %get-tuple-element.41, s32[1]{0:T(128)} %get-tuple-element.38, bf16[512,512]{1,0:T(8,128)(2,1)} %broadcast_select_fusion.2, bf16[16,512,256]{2,1,0:T(8,128)(2,1)} %param.48), custom_call_target="tpu_custom_call" | custom-call | flops 134217728 | bytes 5242944 | tf_op jit(solution)/shard_map/ragged_dot_general/ragged-dot-none
  307.9 9.1 %ragged-dot-none.8 = f32[512,256]{1,0:T(8,128)} custom-call(s32[1]{0:T(128)} %get-tuple-element.38, s32[17]{0:T(128)} %get-tuple-element.39, s32[17]{0:T(128)} %get-tuple-element.40, s32[17]{0:T(128)} %get-tuple-element.41, s32[1]{0:T(128)} %get-tuple-element.38, bf16[512,512]{1,0:T(8,128)(2,1)} %broadcast_select_fusion.2, bf16[16,512,256]{2,1,0:T(8,128)(2,1)} %param.47), custom_call_target="tpu_custom_call" | custom-call | flops 134217728 | bytes 5242944 | tf_op jit(solution)/shard_map/ragged_dot_general/ragged-dot-none
  318.9 9.3 %ragged-dot-none.6 = f32[512,512]{1,0:T(8,128)} custom-call(s32[1]{0:T(128)} %get-tuple-element.38, s32[17]{0:T(128)} %get-tuple-element.39, s32[17]{0:T(128)} %get-tuple-element.40, s32[17]{0:T(128)} %get-tuple-element.41, s32[1]{0:T(128)} %get-tuple-element.38, bf16[512,256]{1,0:T(8,128)(2,1)} %multiply_convert_fusion.2, bf16[16,256,512]{2,1,0:T(8,128)(2,1)} %param.49), custom_call_target="tpu_custom_call" | custom-call | flops 134217728 | bytes 5505088 | tf_op jit(solution)/shard_map/ragged_dot_general/ragged-dot-none
  328.2 4.6 %scatter_custom_fusion.3 = f32[512,512]{1,0:T(8,128)S(1)} fusion(s32[512]{0:T(512)S(1)} %copy-done.40, f32[512,512]{1,0:T(8,128)} %ragged-dot-none.6, f32[512]{0:T(512)S(1)} %get-tuple-element.99, f32[]{:T(128)} %constant.118.clone.1), kind=kCustom, calls=%fused_computation.107 | custom fusion | flops 524288 | bytes 2099204 | tf_op jit(solution)/shard_map/scatter-add | solution.py:68
  334.6 13.7 %ragged-dot-none.9 = f32[512,512]{1,0:T(8,128)} custom-call(s32[1]{0:T(128)} %get-tuple-element.50, s32[17]{0:T(128)} %get-tuple-element.51, s32[17]{0:T(128)} %get-tuple-element.52, s32[17]{0:T(128)} %get-tuple-element.53, s32[1]{0:T(128)} %get-tuple-element.50, bf16[512,256]{1,0:T(8,128)(2,1)} %multiply_convert_fusion.3, bf16[16,256,512]{2,1,0:T(8,128)(2,1)} %param.49), custom_call_target="tpu_custom_call" | custom-call | flops 134217728 | bytes 5505088 | tf_op jit(solution)/shard_map/ragged_dot_general/ragged-dot-none
  348.3 4.6 %scatter_custom_fusion.1 = f32[512,512]{1,0:T(8,128)S(1)} fusion(s32[512]{0:T(512)S(1)} %copy-done.38, f32[512,512]{1,0:T(8,128)} %ragged-dot-none.9, f32[512]{0:T(512)S(1)} %get-tuple-element.97, f32[]{:T(128)} %constant.118.clone.1), kind=kCustom, calls=%fused_computation.110 | custom fusion | flops 524288 | bytes 2099204 | tf_op jit(solution)/shard_map/scatter-add | solution.py:68
  354.6 10.3 %ragged-dot-none.3 = f32[512,512]{1,0:T(8,128)} custom-call(s32[1]{0:T(128)} %get-tuple-element.26, s32[17]{0:T(128)} %get-tuple-element.27, s32[17]{0:T(128)} %get-tuple-element.28, s32[17]{0:T(128)} %get-tuple-element.29, s32[1]{0:T(128)} %get-tuple-element.26, bf16[512,256]{1,0:T(8,128)(2,1)} %multiply_convert_fusion.1, bf16[16,256,512]{2,1,0:T(8,128)(2,1)} %param.49), custom_call_target="tpu_custom_call" | custom-call | flops 134217728 | bytes 5505088 | tf_op jit(solution)/shard_map/ragged_dot_general/ragged-dot-none
  364.9 4.6 %scatter_custom_fusion.5 = f32[512,512]{1,0:T(8,128)S(1)} fusion(s32[512]{0:T(512)S(1)} %get-tuple-element.12, f32[512,512]{1,0:T(8,128)} %ragged-dot-none.3, f32[512]{0:T(512)S(1)} %get-tuple-element.101, f32[]{:T(128)} %constant.118.clone.1), kind=kCustom, calls=%fused_computation.104 | custom fusion | flops 524288 | bytes 2099204 | tf_op jit(solution)/shard_map/scatter-add | solution.py:68
  371.3 8.7 %ragged-dot-none = f32[512,512]{1,0:T(8,128)} custom-call(s32[1]{0:T(128)} %get-tuple-element.14, s32[17]{0:T(128)} %get-tuple-element.15, s32[17]{0:T(128)} %get-tuple-element.16, s32[17]{0:T(128)} %get-tuple-element.17, s32[1]{0:T(128)} %get-tuple-element.14, bf16[512,256]{1,0:T(8,128)(2,1)} %multiply_convert_fusion, bf16[16,256,512]{2,1,0:T(8,128)(2,1)} %param.49), custom_call_target="tpu_custom_call" | custom-call | flops 134217728 | bytes 5505088 | tf_op jit(solution)/shard_map/ragged_dot_general/ragged-dot-none
  380.0 5.5 %scatter_custom_fusion.7 = f32[512,512]{1,0:T(8,128)} fusion(s32[512]{0:T(512)S(1)} %copy-done.36, f32[512,512]{1,0:T(8,128)} %ragged-dot-none, f32[512]{0:T(512)S(1)} %get-tuple-element.103, f32[]{:T(128)} %constant.118.clone.1), kind=kCustom, calls=%fused_computation.101 | custom fusion | flops 524288 | bytes 2099204 | tf_op jit(solution)/shard_map/scatter-add | solution.py:68
  389.4 60.4 %all-reduce.9.cloned.1.call-done = (bf16[512,512]{1,0:T(8,128)(2,1)}, bf16[512,512]{1,0:T(8,128)(2,1)}, bf16[512,512]{1,0:T(8,128)(2,1)}, bf16[512,512]{1,0:T(8,128)(2,1)}) async-done(((bf16[512,512]{1,0:T(8,128)(2,1)}, bf16[512,512]{1,0:T(8,128)(2,1)}, bf16[512,512]{1,0:T(8,128)(2,1)}, bf16[512,512]{1,0:T(8,128)(2,1)}), (bf16[512,512]{1,0:T(8,128)(2,1)}, bf16[512,512]{1,0:T(8,128)(2,1)}, ...) | async-done | bytes 2097168 | tf_op jit(solution)/shard_map/psum | solution.py:69
  (251 shorter events, 115.8 us)
Async XLA Ops:
  7.2 114.0 %copy-start = (bf16[128,512]{1,0:T(8,128)(2,1)S(1)}, bf16[128,512]{1,0:T(8,128)(2,1)}, u32[]{:S(2)}) copy-start(bf16[128,512]{1,0:T(8,128)(2,1)} %param.44) | copy-start | bytes 393220
  7.2 76.6 %all-reduce.7.cloned.1.call-start = ((), (), s32[]{:S(2)}) async-start(), calls=%async_computation | async-start | bytes 1048576 | tf_op jit(solution)/shard_map/psum | solution.py:46
  25.7 158.9 %all-reduce.11.cloned.1.call-start = ((), (), s32[]{:S(2)}) async-start(), calls=%async_computation.2 | async-start | bytes 4194304 | tf_op jit(solution)/shard_map/psum | solution.py:54
  36.0 58.5 %copy-start.39 = (s32[512]{0:T(512)}, s32[512]{0:T(512)S(1)}, u32[]{:S(2)}) copy-start(s32[512]{0:T(512)S(1)} %get-tuple-element.11) | copy-start | bytes 6148
  40.4 54.1 %copy-start.35 = (s32[512]{0:T(512)}, s32[512]{0:T(512)S(1)}, u32[]{:S(2)}) copy-start(s32[512]{0:T(512)S(1)} %get-tuple-element.13) | copy-start | bytes 6148
  94.5 11.9 %copy-start.46 = (f32[512]{0:T(512)S(1)}, f32[512]{0:T(512)}, u32[]{:S(2)}) copy-start(f32[512]{0:T(512)} %add_rsqrt_fusion.13) | copy-start | bytes 6148
  94.5 11.9 %copy-start.50 = (f32[32]{0:T(128)S(1)}, f32[32]{0:T(128)}, u32[]{:S(2)}) copy-start(f32[32]{0:T(128)} %convert_element_type.322) | copy-start | bytes 388
  107.7 13.5 %copy-start.24 = (bf16[512,128]{1,0:T(8,128)(2,1)S(1)}, bf16[512,128]{1,0:T(8,128)(2,1)}, u32[]{:S(2)}) copy-start(bf16[512,128]{1,0:T(8,128)(2,1)} %copy-done.23) | copy-start | bytes 393220
  107.7 13.5 %copy-start.30 = (bf16[512,1,128]{2,0,1:T(8,128)(2,1)S(1)}, bf16[512,1,128]{2,0,1:T(8,128)(2,1)}, u32[]{:S(2)}) copy-start(bf16[512,1,128]{2,0,1:T(8,128)(2,1)} %copy.55) | copy-start | bytes 393220
  107.7 13.5 %copy-start.49 = (f32[128]{0:T(128)S(1)}, f32[128]{0:T(128)}, u32[]{:S(2)}) copy-start(f32[128]{0:T(128)} %param.43) | copy-start | bytes 1540
  107.7 14.7 %copy-start.22 = (bf16[512,128]{1,0:T(8,128)(2,1)S(1)}, bf16[512,128]{1,0:T(8,128)(2,1)}, u32[]{:S(2)}) copy-start(bf16[512,128]{1,0:T(8,128)(2,1)} %copy-done.21) | copy-start | bytes 393220
  107.7 14.7 %copy-start.29 = (bf16[512,1,128]{2,0,1:T(8,128)(2,1)S(1)}, bf16[512,1,128]{2,0,1:T(8,128)(2,1)}, u32[]{:S(2)}) copy-start(bf16[512,1,128]{2,0,1:T(8,128)(2,1)} %copy.52) | copy-start | bytes 393220
  107.7 15.8 %copy-start.20 = (bf16[512,128]{1,0:T(8,128)(2,1)S(1)}, bf16[512,128]{1,0:T(8,128)(2,1)}, u32[]{:S(2)}) copy-start(bf16[512,128]{1,0:T(8,128)(2,1)} %copy-done.19) | copy-start | bytes 393220
  107.7 15.8 %copy-start.28 = (bf16[512,1,128]{2,0,1:T(8,128)(2,1)S(1)}, bf16[512,1,128]{2,0,1:T(8,128)(2,1)}, u32[]{:S(2)}) copy-start(bf16[512,1,128]{2,0,1:T(8,128)(2,1)} %copy.54) | copy-start | bytes 393220
  121.2 31.0 %copy-start.45 = (s32[1,512,1]{1,2,0:T(1,128)S(1)}, s32[1,512,1]{1,2,0:T(1,128)}, u32[]{:S(2)}) copy-start(s32[1,512,1]{1,2,0:T(1,128)} %get-tuple-element.149) | copy-start | bytes 6148
  121.2 34.8 %copy-start.33 = (s32[512]{0:T(512)S(1)}, s32[512]{0:T(512)}, u32[]{:S(2)}) copy-start(s32[512]{0:T(512)} %compare_select_fusion.8) | copy-start | bytes 6148
  121.2 34.8 %copy-start.41 = (s32[512,1,1]{0,2,1:T(1,128)S(1)}, s32[512,1,1]{0,2,1:T(1,128)}, u32[]{:S(2)}) copy-start(s32[512,1,1]{0,2,1:T(1,128)} %get-tuple-element.138) | copy-start | bytes 6148
  121.2 34.8 %copy-start.42 = (s32[512,1,1]{0,2,1:T(1,128)S(1)}, s32[512,1,1]{0,2,1:T(1,128)}, u32[]{:S(2)}) copy-start(s32[512,1,1]{0,2,1:T(1,128)} %get-tuple-element.141) | copy-start | bytes 6148
  121.2 34.8 %copy-start.43 = (s32[512,1,1]{0,2,1:T(1,128)S(1)}, s32[512,1,1]{0,2,1:T(1,128)}, u32[]{:S(2)}) copy-start(s32[512,1,1]{0,2,1:T(1,128)} %get-tuple-element.143) | copy-start | bytes 6148
  121.2 34.8 %copy-start.44 = (s32[512,1,1]{0,2,1:T(1,128)S(1)}, s32[512,1,1]{0,2,1:T(1,128)}, u32[]{:S(2)}) copy-start(s32[512,1,1]{0,2,1:T(1,128)} %get-tuple-element.145) | copy-start | bytes 6148
  125.8 324.0 %all-reduce.9.cloned.1.call-start = ((), (), s32[]{:S(2)}) async-start(), calls=%async_computation.1 | async-start | bytes 4194304 | tf_op jit(solution)/shard_map/psum | solution.py:69
  194.1 18.3 %copy-start.31 = (s32[4,512,1]{1,2,0:T(1,128)S(1)}, s32[4,512,1]{1,2,0:T(1,128)}, u32[]{:S(2)}) copy-start(s32[4,512,1]{1,2,0:T(1,128)} %param.31) | copy-start | bytes 24580
  203.2 16.2 %copy-start.36 = (s32[512]{0:T(512)S(1)}, s32[512]{0:T(512)}, u32[]{:S(2)}) copy-start(s32[512]{0:T(512)} %copy-done.35) | copy-start | bytes 6148
  220.3 17.4 %copy-start.17 = (bf16[512,512]{1,0:T(8,128)(2,1)S(1)}, bf16[512,512]{1,0:T(8,128)(2,1)}, u32[]{:S(2)}) copy-start(bf16[512,512]{1,0:T(8,128)(2,1)} %gather_fusion.6) | copy-start | bytes 1572868
  238.7 19.9 %copy-start.32 = (s32[1024]{0:T(1024)S(1)}, s32[1024]{0:T(1024)}, u32[]{:S(2)}) copy-start(s32[1024]{0:T(1024)} %pad_clamp_fusion.3) | copy-start | bytes 12292
  318.9 14.8 %copy-start.14 = (f32[512,256]{1,0:T(8,128)S(1)}, f32[512,256]{1,0:T(8,128)}, u32[]{:S(2)}) copy-start(f32[512,256]{1,0:T(8,128)} %ragged-dot-none.10) | copy-start | bytes 1572868
  318.9 14.8 %copy-start.15 = (f32[512,256]{1,0:T(8,128)S(1)}, f32[512,256]{1,0:T(8,128)}, u32[]{:S(2)}) copy-start(f32[512,256]{1,0:T(8,128)} %ragged-dot-none.11) | copy-start | bytes 1572868
  334.6 19.2 %copy-start.12 = (f32[512,256]{1,0:T(8,128)S(1)}, f32[512,256]{1,0:T(8,128)}, u32[]{:S(2)}) copy-start(f32[512,256]{1,0:T(8,128)} %ragged-dot-none.4) | copy-start | bytes 1572868
  334.6 19.2 %copy-start.13 = (f32[512,256]{1,0:T(8,128)S(1)}, f32[512,256]{1,0:T(8,128)}, u32[]{:S(2)}) copy-start(f32[512,256]{1,0:T(8,128)} %ragged-dot-none.5) | copy-start | bytes 1572868
  354.6 15.8 %copy-start.10 = (f32[512,256]{1,0:T(8,128)S(1)}, f32[512,256]{1,0:T(8,128)}, u32[]{:S(2)}) copy-start(f32[512,256]{1,0:T(8,128)} %ragged-dot-none.1) | copy-start | bytes 1572868
  354.6 15.8 %copy-start.11 = (f32[512,256]{1,0:T(8,128)S(1)}, f32[512,256]{1,0:T(8,128)}, u32[]{:S(2)}) copy-start(f32[512,256]{1,0:T(8,128)} %ragged-dot-none.2) | copy-start | bytes 1572868
  380.0 69.8 %copy-start.4 = (bf16[4,512,512]{2,1,0:T(8,128)(2,1)S(1)}, bf16[4,512,512]{2,1,0:T(8,128)(2,1)}, u32[]{:S(2)}) copy-start(bf16[4,512,512]{2,1,0:T(8,128)(2,1)} %param.28) | copy-start | bytes 6291460
  (22 other events, 87.0 us)
Sparse Core Ops, SparseCore 0:
  25.8 57.9 all-reduce.6
  125.9 58.6 all-reduce.10
  388.3 66.2 all-reduce.8
where the time goes:
time: 471 us; the launch traced here: 461 us
  Pallas kernels  132 us (28%)
  waiting for transfers between devices  124 us (26%)
  other arithmetic  114 us (24%)
  local copies, waits for them, and re-layouts  60.6 us (13%)
  matrix products  19 us (4%)
  between operations  15.3 us (3%)
    another operation x12, Pallas kernels  125 us
    psum x1, waiting for transfers between devices, layer_steps(): moe_sum = lax.psum(moe_part.astype(jnp.bfloat16), 'tp')  64.7 us
    psum x1, waiting for transfers between devices, layer_steps(): lax.psum(jnp.dot(x_conv, w_xp, preferred_element_type=jnp.float32), 'tp')  31.2 us
    psum x1, waiting for transfers between devices, layer_steps(): lax.psum(jnp.dot(y_gated, w_out, preferred_element_type=jnp.float32).asty...  28.5 us
    scatter-add x4, other arithmetic, layer_steps(): jax.ops.segment_sum(y_rows * gate_rows[:, None], tok_rows, num_segments=b...  19.4 us
    scatter-add x4, other arithmetic, layer_steps(): counts = jnp.bincount(flat_ids, length=experts).astype(jnp.int32)  19.1 us
    gather x4, local copies, waits for them, and re-layouts, layer_steps(): jnp.take_along_axis(route_prob, ids_now, axis=1).reshape(route_rows)  18.2 us
    sort x4, other arithmetic, layer_steps(): sort_order = jnp.argsort(flat_ids, stable=True)  15.1 us
  transfers between devices with their start and end apart: 3, of which 3 were waited for; matrix products, arithmetic and copies ran while one was open for 11% of the time, Pallas kernels for 2%

commit v1 on v0

v1 whole, which is shorter than its diff:
```python
import functools

import jax
import jax.numpy as jnp
from jax import lax
from jax.experimental import pallas as pl
from jax.experimental.pallas import tpu as pltpu
from jax.sharding import PartitionSpec as P

EPSILON = 1e-6
LOG2E = 1.4426950408889634
MESH = pl.DeviceIdType.MESH
BF = jnp.bfloat16
F32 = jnp.float32
NT = (((1,), (1,)), ((), ()))


def sigmoid(v):
    return 1.0 / (1.0 + jnp.exp(-v))


def layer_kernel(cfg, x_hbm, conv_hbm, ssm_hbm, ids_ref, vec_ref, win_ref, convw_ref, wxpt_ref, wdt_ref, alogt_ref, wout_ref, wrt_ref,
                 wg_hbm, wu_hbm, wd_hbm, y_hbm, convo_hbm, ssmo_hbm,
                 xv, seq, hst, wg, wu, wd, winp, w2t, wdt2, a2, nbuf, zbuf, xcb, idsb, ppk, prx, ptx, prs, pn, delta, dxb, ygb,
                 ypart, yrx, ytx1, ytxd, ytx2, yrx1, yrxd, yrx2, opart, orx, otx1, otxd, otx2, orx1, orxd, orx2,
                 ubuf, pwb, mfull, yfull, hid, lsem, ssem, rsem):
    S, Bt, D, C, N, R, E, F = cfg["S"], cfg["B"], cfg["D"], cfg["C"], cfg["N"], cfg["R"], cfg["E"], cfg["F"]
    chips = cfg["chips"]
    half, quarter = Bt // 2, Bt // 8
    eighth = quarter // 2
    phalf, pquart = Bt // 4, Bt // 16

    t = lax.axis_index("tp")
    q = t // 2
    c = t % 2
    dev = lambda chip, core: (chip % chips) * 2 + core
    right, left, opp, partner = dev(q + 1, c), dev(q + chips - 1, c), dev(q + 2, c), q * 2 + (1 - c)
    q_r, q_l, q_o = (q + 1) % chips, (q + chips - 1) % chips, (q + 2) % chips

    lcount = [0]

    def local(src, dst):
        cp = pltpu.make_async_copy(src, dst, lsem.at[lcount[0]])
        lcount[0] += 1
        cp.start()
        return cp

    ld_x = [local(x_hbm.at[s], xv.at[s]) for s in range(S)]
    ld_conv = local(conv_hbm, seq.at[pl.ds(0, 3)])
    ld_h = [local(ssm_hbm.at[:, n, :], hst.at[n]) for n in range(N)]
    ld_w = [local(wg_hbm, wg), local(wu_hbm, wu), local(wd_hbm, wd)]

    barrier = pltpu.get_barrier_semaphore()
    for peer in (partner, right, left, opp):
        pl.semaphore_signal(barrier, inc=1, device_id={"tp": peer}, device_id_type=MESH)

    keys = {}

    def remote(key, src, dst, peer):
        i = keys.setdefault(key, len(keys))
        cp = pltpu.make_async_remote_copy(src_ref=src, dst_ref=dst, send_sem=ssem.at[i], recv_sem=rsem.at[i],
                                          device_id={"tp": peer}, device_id_type=MESH)
        cp.start()
        live[key] = cp

    live = {}

    def got(*ks):
        for k in ks:
            live[k].wait_recv()

    g_in = vec_ref[0:1, :]
    g_ff = vec_ref[1:2, :]
    g_p = vec_ref[2:3, 0:C]
    conv_b = vec_ref[2:3, C:2 * C]
    b_dt = vec_ref[2:3, 2 * C:3 * C]
    d_skip = vec_ref[2:3, 3 * C:4 * C]

    ri = lax.broadcasted_iota(jnp.int32, (2 * C, 2 * C), 0)
    ci = lax.broadcasted_iota(jnp.int32, (2 * C, 2 * C), 1)
    src_row = jnp.where(ri < C, 2 * ri, 2 * (ri - C) + 1)
    perm = (ci == src_row).astype(BF)
    for blk in range(D // C):
        deint = jnp.dot(perm, win_ref[pl.ds(blk * 2 * C, 2 * C), :], preferred_element_type=F32).astype(BF)
        winp[pl.ds(blk * C, C), 0:C] = deint[0:C]
        winp[pl.ds(blk * C, C), C:2 * C] = deint[C:2 * C]
    PW = R + 2 * N
    w2t[...] = jnp.zeros_like(w2t)
    w2t[0:PW, 0:C] = wxpt_ref[...]
    w2t[PW:2 * PW, C:2 * C] = wxpt_ref[...]
    wdt2[...] = jnp.zeros_like(wdt2)
    wdt2[0:R, 0:C] = wdt_ref[...]
    wdt2[PW:PW + R, C:2 * C] = wdt_ref[...]
    a2[...] = -jnp.exp(alogt_ref[...]) * LOG2E
    for s in range(S):
        row = ids_ref[s].astype(F32)
        idsb[s] = jnp.transpose(jnp.broadcast_to(row, (C, Bt)))

    def rms_rows(v, gain):
        return v * lax.rsqrt(jnp.mean(v * v, axis=-1, keepdims=True) + EPSILON) * gain

    def stage_a(s):
        ld_x[s].wait()
        if s == 0:
            ld_conv.wait()

        def norm_body(i, _):
            rows = pl.ds(pl.multiple_of(i * 64, 64), 64)
            nbuf[rows, :] = rms_rows(xv[s, rows, :].astype(F32), g_in).astype(BF)
            return 0

        lax.fori_loop(0, Bt // 64, norm_body, 0)

        def proj_body(i, _):
            rows = pl.ds(pl.multiple_of(i * 128, 128), 128)
            xz = jnp.dot(nbuf[rows, :], winp[...], preferred_element_type=F32).astype(BF)
            seq[3 + s, rows, :] = xz[:, 0:C]
            zbuf[s, rows, :] = xz[:, C:2 * C]
            acc = xz[:, 0:C].astype(F32) * convw_ref[3:4, :].astype(F32) + conv_b
            for j in range(3):
                acc = acc + seq[s + j, rows, :].astype(F32) * convw_ref[j:j + 1, :].astype(F32)
            xcb[s, rows, :] = (acc * sigmoid(acc)).astype(BF)
            return 0

        lax.fori_loop(0, Bt // 128, proj_body, 0)
        xc2 = jnp.concatenate([xcb[s, 0:half, :], xcb[s, half:Bt, :]], axis=1)
        ppk[s] = lax.dot_general(xc2, w2t[...], NT, preferred_element_type=F32)
        if s == 0:
            pl.semaphore_wait(barrier, 4)
        mine = pl.ds(pl.multiple_of((1 - c) * phalf, phalf), phalf)
        remote(("p0", s), ppk.at[s, mine], prx.at[s], partner)

    def p_rows(j):
        return pl.ds(pl.multiple_of(c * phalf + j * pquart, pquart), pquart)

    def stage_p1(s):
        got(("p0", s))
        ptx[s] = ppk[s, pl.ds(pl.multiple_of(c * phalf, phalf), phalf), :] + prx[s]
        for k, (peer, j) in enumerate(((right, q_r), (left, q_l), (opp, q_o))):
            src = ptx.at[s, pl.ds(pl.multiple_of(j * pquart, pquart), pquart)]
            remote(("p1", s, k), src, prs.at[s, k], peer)

    def stage_p2(s):
        got(*[("p1", s, k) for k in range(3)])
        v = ptx[s, pl.ds(pl.multiple_of(q * pquart, pquart), pquart), :] + prs[s, 0] + prs[s, 1] + prs[s, 2]
        lane = lax.broadcasted_iota(jnp.int32, v.shape, 1)
        sq = v * v
        scale = jnp.zeros_like(v)
        for base in (0, PW):
            for lo, width in ((0, R), (R, N), (R + N, N)):
                inside = (lane >= base + lo) & (lane < base + lo + width)
                ms = jnp.sum(jnp.where(inside, sq, 0.0), axis=-1, keepdims=True) * (1.0 / width)
                scale = jnp.where(inside, lax.rsqrt(ms + EPSILON), scale)
        pn[s, p_rows(q), :] = v * scale * g_p
        for k, peer in enumerate((right, left, opp)):
            remote(("p2", s, k), pn.at[s, p_rows(q)], pn.at[s, p_rows(q)], peer)

    def stage_p3(s):
        got(*[("p2", s, k) for k in range(3)])
        own = pl.ds(pl.multiple_of(c * phalf, phalf), phalf)
        remote(("p3", s), pn.at[s, own], pn.at[s, own], partner)

    def stage_ssm(s):
        got(("p3", s))
        if s == 0:
            for cp in ld_h:
                cp.wait()
        raw = jnp.dot(pn[s].astype(BF), wdt2[...], preferred_element_type=F32)
        for hf in range(2):
            v = raw[:, hf * C:(hf + 1) * C] + b_dt
            rows = pl.ds(hf * half, half)
            dl = jnp.maximum(v, 0.0) + jnp.log1p(jnp.exp(-jnp.abs(v)))
            delta[rows, :] = dl
            dxb[rows, :] = dl * xcb[s, rows, :].astype(F32)
        blk = 32

        def body(i, _):
            pb = pn[s, pl.ds(pl.multiple_of(i * blk, blk), blk), :]
            for hf in range(2):
                rows = pl.ds(pl.multiple_of(hf * half + i * blk, blk), blk)
                d = delta[rows, :]
                dx = dxb[rows, :]
                acc = d_skip * xcb[s, rows, :].astype(F32)
                for n in range(N):
                    b_col = hf * PW + R + n
                    c_col = b_col + N
                    bb = jnp.broadcast_to(pb[:, b_col:b_col + 1], (blk, C))
                    cc = jnp.broadcast_to(pb[:, c_col:c_col + 1], (blk, C))
                    hn = jnp.exp2(d * a2[n:n + 1, :]) * hst[n, rows, :] + dx * bb
                    hst[n, rows, :] = hn
                    acc = acc + hn * cc
                zf = zbuf[s, rows, :].astype(F32)
                ygb[rows, :] = (acc * (zf * sigmoid(zf))).astype(BF)
            return 0

        lax.fori_loop(0, half // blk, body, 0)

        def out_body(i, _):
            rows = pl.ds(pl.multiple_of(i * 128, 128), 128)
            ypart[s, rows, :] = jnp.dot(ygb[rows, :], wout_ref[...], preferred_element_type=F32).astype(BF)
            return 0

        lax.fori_loop(0, Bt // 128, out_body, 0)
        rs0("y", s)

    bufs = {"y": (ypart, yrx, ytx1, ytxd, ytx2, yrx1, yrxd, yrx2), "o": (opart, orx, otx1, otxd, otx2, orx1, orxd, orx2)}

    def rs0(w, s):
        part, prx_ = bufs[w][0:2]
        src = pl.ds(pl.multiple_of((1 - c) * half, half), half)
        remote((w, 0, s), part.at[s, src], prx_.at[s], partner)

    def chip_sum(w, s, j, hv):
        part, prx_ = bufs[w][0:2]
        a = part[s, pl.ds(pl.multiple_of(c * half + j * quarter + hv * eighth, eighth), eighth), :].astype(F32)
        b = prx_[s, pl.ds(pl.multiple_of(j * quarter + hv * eighth, eighth), eighth), :].astype(F32)
        return a + b

    def rs1(w, s):
        _, _, tx1, txd, _, rx1, rxd, _ = bufs[w]
        got((w, 0, s))
        tx1[s, 0] = chip_sum(w, s, q_o, 0).astype(BF)
        remote((w, 1, s, 0), tx1.at[s, 0], rx1.at[s, 0], right)
        tx1[s, 1] = chip_sum(w, s, q_o, 1).astype(BF)
        remote((w, 1, s, 1), tx1.at[s, 1], rx1.at[s, 1], left)
        txd[s, 0] = chip_sum(w, s, q_r, 1).astype(BF)
        remote((w, 2, s, 0), txd.at[s, 0], rxd.at[s, 0], right)
        txd[s, 1] = chip_sum(w, s, q_l, 0).astype(BF)
        remote((w, 2, s, 1), txd.at[s, 1], rxd.at[s, 1], left)

    def rs2(w, s):
        _, _, _, _, tx2, rx1, _, rx2 = bufs[w]
        got((w, 1, s, 0))
        tx2[s, 0] = (chip_sum(w, s, q_r, 0) + rx1[s, 0].astype(F32)).astype(BF)
        remote((w, 3, s, 0), tx2.at[s, 0], rx2.at[s, 0], right)
        got((w, 1, s, 1))
        tx2[s, 1] = (chip_sum(w, s, q_l, 1) + rx1[s, 1].astype(F32)).astype(BF)
        remote((w, 3, s, 1), tx2.at[s, 1], rx2.at[s, 1], left)

    def rs3(w, s):
        _, _, _, _, _, _, rxd, rx2 = bufs[w]
        got((w, 2, s, 0), (w, 2, s, 1), (w, 3, s, 0), (w, 3, s, 1))
        lo = chip_sum(w, s, q, 0) + rx2[s, 0].astype(F32) + rxd[s, 1].astype(F32)
        hi = chip_sum(w, s, q, 1) + rx2[s, 1].astype(F32) + rxd[s, 0].astype(F32)
        return lo, hi

    def rows_of(j, hv=None):
        if hv is None:
            return pl.ds(pl.multiple_of(c * half + j * quarter, quarter), quarter)
        return pl.ds(pl.multiple_of(c * half + j * quarter + hv * eighth, eighth), eighth)

    def ag1(w, buf, s):
        own = buf.at[s, rows_of(q)]
        remote((w, 0, s, 0), own, own, right)
        remote((w, 0, s, 1), own, own, left)
        remote((w, 1, s, 0), own, own, partner)

    def ag2(w, buf, s):
        got((w, 0, s, 0))
        fwd = buf.at[s, rows_of(q_l, 0)]
        remote((w, 2, s, 0), fwd, fwd, right)
        got((w, 0, s, 1))
        fwd = buf.at[s, rows_of(q_r, 1)]
        remote((w, 2, s, 1), fwd, fwd, left)
        for k, j in enumerate((q_l, q_r)):
            sh = buf.at[s, rows_of(j)]
            remote((w, 1, s, 1 + k), sh, sh, partner)

    def ag3(w, buf, s):
        got((w, 2, s, 0), (w, 2, s, 1))
        sh = buf.at[s, rows_of(q_o)]
        remote((w, 1, s, 3), sh, sh, partner)

    def ag4(w, s):
        got(*[(w, 1, s, k) for k in range(4)])

    def y3(s):
        sums = rs3("y", s)
        for hv in range(2):
            rows = rows_of(q, hv)
            loc = pl.ds(hv * eighth, eighth)
            u = (xv[s, rows, :].astype(F32) + sums[hv]).astype(BF)
            ubuf[s, loc, :] = u
            mfull[s, rows, :] = rms_rows(u.astype(F32), g_ff).astype(BF)
        ag1("m", mfull, s)
        logits = lax.dot_general(mfull[s, rows_of(q), :], wrt_ref[...], NT, preferred_element_type=F32)
        ex = jnp.exp(logits - jnp.max(logits, axis=-1, keepdims=True))
        ids = idsb[s, rows_of(q), :][:, 0:E]
        pick = jnp.where(lax.broadcasted_iota(jnp.int32, ex.shape, 1).astype(F32) == ids, ex, 0.0)
        prob = jnp.sum(pick, axis=-1, keepdims=True) / jnp.sum(ex, axis=-1, keepdims=True)
        pwb[s] = jnp.broadcast_to(prob, (quarter, C))

    def o3(s):
        sums = rs3("o", s)
        for hv in range(2):
            rows = rows_of(q, hv)
            loc = pl.ds(hv * eighth, eighth)
            pw = pwb[s, loc, :][:, 0:1]
            yfull[s, rows, :] = (ubuf[s, loc, :].astype(F32) + pw * sums[hv]).astype(BF)
        ag1("z", yfull, s)

    def moe_part(s, lo, hi):
        def body(e, _):
            m = mfull[s]
            gate = jnp.dot(m, wg[e], preferred_element_type=F32)
            up = jnp.dot(m, wu[e], preferred_element_type=F32)
            act = gate * sigmoid(gate) * up
            keep = idsb[s] == e.astype(F32)
            cols = pl.ds(pl.multiple_of(e * F, F), F)
            hid[:, cols] = jnp.concatenate([jnp.where(keep, act[:, k * C:(k + 1) * C], 0.0) for k in range(F // C)], axis=1).astype(BF)
            return 0

        lax.fori_loop(lo, hi, body, 0)

    def moe_down(s):
        def body(i, _):
            rows = pl.ds(pl.multiple_of(i * 256, 256), 256)
            opart[s, rows, :] = jnp.dot(hid[rows, :], wd[...], preferred_element_type=F32).astype(BF)
            return 0

        lax.fori_loop(0, Bt // 256, body, 0)
        rs0("o", s)

    st_y = []

    def y_out(s):
        ag4("z", s)
        st_y.append(local(yfull.at[s], y_hbm.at[s]))

    acts = {
        "A": stage_a, "p1": stage_p1, "p2": stage_p2, "p3": stage_p3, "S": stage_ssm,
        "y1": lambda s: rs1("y", s), "y2": lambda s: rs2("y", s), "y3": y3,
        "m2": lambda s: ag2("m", mfull, s), "m3": lambda s: ag3("m", mfull, s), "m4": lambda s: ag4("m", s),
        "o1": lambda s: rs1("o", s), "o2": lambda s: rs2("o", s), "o3": o3,
        "z2": lambda s: ag2("z", yfull, s), "z3": lambda s: ag3("z", yfull, s), "z4": y_out, "D": moe_down,
    }
    for k in range(4):
        acts["M%d" % k] = functools.partial(lambda k, s: moe_part(s, k * (E // 4), (k + 1) * (E // 4)), k)

    st_state = []

    def run(*plan):
        for item in plan:
            name, s = item.split(".")
            acts[name](int(s))

    run("A.0", "A.1", "p1.0", "A.2", "p1.1", "A.3", "p2.0", "p1.2", "p2.1", "p3.0", "p1.3", "p2.2", "p3.1", "S.0", "p2.3", "p3.2", "S.1", "y1.0", "p3.3", "S.2", "y2.0", "y1.1", "S.3")
    st_state.append(local(seq.at[pl.ds(S, 3)], convo_hbm))
    for n in range(N):
        st_state.append(local(hst.at[n], ssmo_hbm.at[:, n, :]))
    run("y3.0", "y2.1", "y1.2", "m2.0", "y3.1", "y2.2", "y1.3", "m3.0", "m2.1", "y3.2", "y2.3", "m4.0")
    for cp in ld_w:
        cp.wait()
    run("M0.0", "m3.1", "y3.3", "M1.0", "m2.2", "M2.0", "m3.2", "m2.3", "M3.0", "m3.3", "D.0")
    run("m4.1", "M0.1", "o1.0", "M1.1", "o2.0", "M2.1", "o3.0", "M3.1", "z2.0", "D.1")
    run("m4.2", "M0.2", "z3.0", "o1.1", "M1.2", "z4.0", "o2.1", "M2.2", "o3.1", "M3.2", "z2.1", "D.2")
    run("m4.3", "M0.3", "z3.1", "o1.2", "M1.3", "z4.1", "o2.2", "M2.3", "o3.2", "M3.3", "z2.2", "D.3")
    run("z3.2", "o1.3", "z4.2", "o2.3", "o3.3", "z2.3", "z3.3", "z4.3")
    for cp in live.values():
        cp.wait_send()
    for cp in st_state + st_y:
        cp.wait()


def solution(mesh):
    act_spec = P(None, "dp", None)
    state_spec = P("dp", "tp", None)
    in_specs = (act_spec, state_spec, state_spec, act_spec, P(None), P(None, None, "tp"), P("tp", None), P("tp"), P("tp", None), P(None), P(None), P(None), P(None, "tp"), P("tp"), P("tp", None), P("tp"), P("tp", None), P(None), P(None, None), P(None, None, "tp"), P(None, None, "tp"), P(None, "tp", None))
    out_specs = (act_spec, state_spec, state_spec)
    chips = mesh.shape["tp"] // 2
    assert chips == 4

    def layer_steps(x_steps, conv_state, ssm_state, expert_ids, g_in, w_in, conv_w, conv_b, w_xp, g_dt, g_b, g_c, w_dt, b_dt, a_log, d_skip, w_out, g_ff, w_router, w_gate, w_up, w_down):
        S, B, D = x_steps.shape
        C = w_in.shape[2]
        R = w_dt.shape[0]
        N = a_log.shape[1]
        E, _, F = w_gate.shape
        assert expert_ids.shape[2] == 1 and D == 4 * C and 2 * (R + 2 * N) == C
        cfg = dict(S=S, B=B, D=D, C=C, N=N, R=R, E=E, F=F, chips=chips)
        f = lambda a: a.astype(F32)
        vec = jnp.concatenate([f(g_in), f(g_ff), f(g_dt), f(g_b), f(g_c), f(g_dt), f(g_b), f(g_c), f(conv_b), f(b_dt), d_skip,
                               jnp.zeros((5 * D,), F32)]).reshape(8, D)
        vm = pl.BlockSpec(memory_space=pltpu.VMEM)
        anym = pl.BlockSpec(memory_space=pl.ANY)
        half, quarter, eighth = B // 2, B // 8, B // 16
        ring = lambda: [
            pltpu.VMEM((S, B, D), BF), pltpu.VMEM((S, half, D), BF),
            pltpu.VMEM((S, 2, eighth, D), BF), pltpu.VMEM((S, 2, eighth, D), BF), pltpu.VMEM((S, 2, eighth, D), BF),
            pltpu.VMEM((S, 2, eighth, D), BF), pltpu.VMEM((S, 2, eighth, D), BF), pltpu.VMEM((S, 2, eighth, D), BF)]
        n_remote = S * (8 + 2 * 7 + 2 * 8)
        scratch = [
            pltpu.VMEM((S, B, D), BF), pltpu.VMEM((3 + S, B, C), BF), pltpu.VMEM((N, B, C), F32),
            pltpu.VMEM((E, D, F), BF), pltpu.VMEM((E, D, F), BF), pltpu.VMEM((E * F, D), BF),
            pltpu.VMEM((D, 2 * C), BF), pltpu.VMEM((C, 2 * C), BF), pltpu.VMEM((C, 2 * C), BF), pltpu.VMEM((N, C), F32),
            pltpu.VMEM((B, D), BF), pltpu.VMEM((S, B, C), BF), pltpu.VMEM((S, B, C), BF), pltpu.VMEM((S, B, C), F32),
            pltpu.VMEM((S, half, C), F32), pltpu.VMEM((S, half // 2, C), F32), pltpu.VMEM((S, half // 2, C), F32),
            pltpu.VMEM((S, 3, B // 16, C), F32), pltpu.VMEM((S, half, C), F32),
            pltpu.VMEM((B, C), F32), pltpu.VMEM((B, C), F32), pltpu.VMEM((B, C), BF),
            *ring(), *ring(),
            pltpu.VMEM((S, quarter, D), BF), pltpu.VMEM((S, quarter, C), F32),
            pltpu.VMEM((S, B, D), BF), pltpu.VMEM((S, B, D), BF), pltpu.VMEM((B, E * F), BF),
            pltpu.SemaphoreType.DMA((2 * S + 2 + 2 * N + 3,)),
            pltpu.SemaphoreType.DMA((n_remote,)), pltpu.SemaphoreType.DMA((n_remote,)),
        ]
        y, conv_o, ssm_o = pl.pallas_call(
            functools.partial(layer_kernel, cfg),
            out_shape=(jax.ShapeDtypeStruct((S, B, D), BF), jax.ShapeDtypeStruct((3, B, C), BF), jax.ShapeDtypeStruct((B, N, C), F32)),
            in_specs=[anym, anym, anym, vm, vm, vm, vm, vm, vm, vm, vm, vm, anym, anym, anym],
            out_specs=(anym, anym, anym),
            scratch_shapes=scratch,
            compiler_params=pltpu.CompilerParams(collective_id=0, has_side_effects=True, vmem_limit_bytes=62 * 1024 * 1024),
            name="layer_steps",
        )(x_steps, conv_state.transpose(2, 0, 1), ssm_state.transpose(0, 2, 1), expert_ids.transpose(0, 2, 1), vec,
          w_in.reshape(2 * D, C), conv_w.T, w_xp.T, w_dt, a_log.T, w_out, w_router.T, w_gate, w_up, w_down.reshape(E * F, D))
        return y, conv_o.transpose(1, 2, 0), ssm_o.transpose(0, 2, 1)

    return jax.shard_map(layer_steps, mesh=mesh, in_specs=in_specs, out_specs=out_specs, check_vma=False)
```

time: 471 us -> 145 us (0.31); the launches traced: 461 us -> 142 us
  waiting for transfers between devices: 124 us -> 0 us
  other arithmetic: 114 us -> 0 us
  local copies, waits for them, and re-layouts: 60.6 us -> 15.1 us
  matrix products: 19 us -> 0 us
  between operations: 15.3 us -> 0.66 us
  Pallas kernels: 132 us -> 127 us
    pallas_call x0 -> x1, Pallas kernels: none -> 127 us  [layer_steps(): pl.pallas_call(functools.partial(layer_kernel, cfg), out_shape=(jax.Shape...]
    another operation x12 -> x0, Pallas kernels: 125 us -> none
    psum x3 -> x0, waiting for transfers between devices: 124 us -> none  [the longest x1 64.7 us: layer_steps(): moe_sum = lax.psum(moe_part.astype(jnp.bfloat16), 'tp')]
    gather x12 -> x0, local copies, waits for them, and re-layouts: 40.7 us -> none  [the longest x4 18.2 us: layer_steps(): jnp.take_along_axis(route_prob, ids_now, axis=1).reshape(route_rows)]
    scatter-add x8 -> x0, other arithmetic: 38.6 us -> none  [the longest x4 19.4 us: layer_steps(): jax.ops.segment_sum(y_rows * gate_rows[:, None], tok_rows, num_segments=b...]
    reduce_sum x16 -> x0, other arithmetic: 25 us -> none  [the longest x1 13.4 us: layer_steps(): jnp.sum(ssm_st * c_vec[:, None, :], axis=2) + d_skip[None] * xc_f32]
    dot_general x20 -> x0, matrix products: 19 us -> none  [the longest x4 5.44 us: layer_steps(): jnp.dot(dt_low.astype(jnp.bfloat16), w_dt, preferred_element_type=jnp.flo...]
    convert_element_type x18 -> x0, other arithmetic: 17.3 us -> none  [the longest x4 4.7 us: layer_steps(): moe_sum = lax.psum(moe_part.astype(jnp.bfloat16), 'tp')]
  transfers between devices with their start and end apart: 3 -> 0, of which waited for: 3 -> 0; matrix products, arithmetic and copies ran while one was open for 11% -> 0% of each run, Pallas kernels for 2% -> 0%
where the time goes in v1:
time: 145 us; the launch traced here: 142 us
  Pallas kernels  127 us (88%)
  local copies, waits for them, and re-layouts  15.1 us (10%)
    pallas_call x1, Pallas kernels, layer_steps(): pl.pallas_call(functools.partial(layer_kernel, cfg), out_shape=(jax.Shape...  127 us
    concatenate x1, local copies, waits for them, and re-layouts, layer_steps(): jnp.concatenate([f(g_in), f(g_ff), f(g_dt), f(g_b), f(g_c), f(g_dt), f(g_...  7.46 us
    unnamed x5, local copies, waits for them, and re-layouts  6.99 us

profile of v1, /device:TPU:80, one launch (start us, length us, event | category | flops | bytes accessed | tf_op | source)
XLA Modules:
  0.0 142.4 jit_solution(841172273100147716)
XLA Ops:
  0.6 7.5 %concatenate.3 = f32[4096]{0:T(1024)S(1)} concatenate(bf16[512]{0:T(512)(128)(2,1)} %param.26, bf16[512]{0:T(512)(128)(2,1)} %param.39, bf16[32]{0:T(256)(128)(2,1)} %param.31, bf16[16]{0:T(256)(128)(2,1)} %param.32, bf16[16]{0:T(256)(128)(2,1)} %param.33, bf16[32]{0:T(256)(128)(2,1)} %param.31, bf16[16]{0:T(256)(128)(2,1)} %param.32, bf16[16]{0:T(256)(128)(2,1)} %param.33, ...), dimensions={0} | concatenate | bytes 29952 | tf_op jit(solution)/shard_map/concatenate | solution.py:382
  8.1 0.6 reshape.15.vec_ref
  8.7 126.7 %layer_steps.1 = (bf16[4,512,512]{2,1,0:T(8,128)(2,1)}, bf16[3,512,128]{2,1,0:T(8,128)(2,1)}, f32[512,16,128]{2,1,0:T(8,128)}) custom-call(bf16[4,512,512]{2,1,0:T(8,128)(2,1)} %x_hbm.1, bf16[3,512,128]{2,1,0:T(8,128)(2,1)} %bitcast.15, f32[512,16,128]{2,1,0:T(8,128)} %bitcast.12, s32[4,1,512]{2,1,0:T(1,128)} %bitcast.19, f32[8,512]{1,0:T(8,128)} %reshape.15.vec_ref, ...), custom_call_target="tpu_custom_call" | custom-call | tf_op jit(solution)/shard_map/layer_steps/pallas_call | solution.py:406
  135.4 0.0 copy-start
  135.4 3.2 %copy.28 = bf16[4,512,512]{2,1,0:T(8,128)(2,1)} copy(bf16[4,512,512]{2,1,0:T(8,128)(2,1)} %get-tuple-element.12) | data formatting | bytes 4194304
  138.6 1.8 %copy.29 = bf16[512,128,3]{1,0,2:T(8,128)(2,1)} copy(bf16[512,128,3]{1,0,2:T(8,128)(2,1)} %bitcast.14) | data formatting | bytes 786432
  140.4 0.0 copy-done
  140.4 2.0 %copy.30 = f32[512,128,16]{1,2,0:T(8,128)} copy(f32[512,128,16]{1,2,0:T(8,128)S(1)} %bitcast.11) | data formatting | bytes 8388608
  (1 shorter events, 0.0 us)
Async XLA Ops:
  135.4 5.0 %copy-start = (f32[512,16,128]{2,1,0:T(8,128)S(1)}, f32[512,16,128]{2,1,0:T(8,128)}, u32[]{:S(2)}) copy-start(f32[512,16,128]{2,1,0:T(8,128)} %get-tuple-element.8) | copy-start | bytes 12582916

commit v2 on v1

v2 whole, which is shorter than its diff:
```python
import functools

import jax
import jax.numpy as jnp
from jax import lax
from jax.experimental import pallas as pl
from jax.experimental.pallas import tpu as pltpu
from jax.sharding import PartitionSpec as P

EPSILON = 1e-6
LOG2E = 1.4426950408889634
MESH = pl.DeviceIdType.MESH
BF = jnp.bfloat16
F32 = jnp.float32
NT = (((1,), (1,)), ((), ()))


def silu(v):
    h = 0.5 * v
    return h + h * jnp.tanh(h)


def layer_kernel(cfg, x_hbm, conv_hbm, ssm_hbm, tt_ref, ids_ref, gin_ref, gff_ref, gdt_ref, gb_ref, gc_ref, win_ref, convw_ref, convb_ref,
                 wxpt_ref, wdt_ref, bdt_ref, alogt_ref, dskip_ref, wout_ref, wrt_ref, wg_hbm, wu_hbm, wd_hbm, y_hbm, convo_hbm, ssmo_hbm,
                 xv, cst, seq, hst, wg, wu, wd, wint, ab, cols, gp, nbuf, zbuf, xcb, idsb, rcb, pm, ubig, msort, hbuf, opair,
                 ppk, prx, ptx, prs, pn, delta, dxb, ygb,
                 ypart, yrx, ytx1, ytxd, ytx2, yrx1, yrxd, yrx2, opart, orx, otx1, otxd, otx2, orx1, orxd, orx2,
                 ubuf, pwb, mfull, yfull, lsem, ssem, rsem):
    S, Bt, D, C, N, R, E, F = cfg["S"], cfg["B"], cfg["D"], cfg["C"], cfg["N"], cfg["R"], cfg["E"], cfg["F"]
    chips, T, tiles, slots = cfg["chips"], cfg["T"], cfg["tiles"], cfg["slots"]
    half, quarter = Bt // 2, Bt // 8
    eighth = quarter // 2
    JB = Bt // C
    PH = R

    t = lax.axis_index("tp")
    q = t // 2
    c = t % 2
    dev = lambda chip, core: (chip % chips) * 2 + core
    right, left, opp, partner = dev(q + 1, c), dev(q + chips - 1, c), dev(q + 2, c), q * 2 + (1 - c)
    q_r, q_l, q_o = (q + 1) % chips, (q + chips - 1) % chips, (q + 2) % chips

    lcount = [0]

    def local(src, dst):
        cp = pltpu.make_async_copy(src, dst, lsem.at[lcount[0]])
        lcount[0] += 1
        cp.start()
        return cp

    ld_x = [local(x_hbm.at[s], xv.at[s]) for s in range(S)]
    ld_conv = local(conv_hbm, cst)
    ld_h = [local(ssm_hbm.at[:, n, :], hst.at[n]) for n in range(N)]
    ld_w = [local(wg_hbm, wg), local(wu_hbm, wu), local(wd_hbm, wd)]

    barrier = pltpu.get_barrier_semaphore()
    for peer in (partner, right, left, opp):
        pl.semaphore_signal(barrier, inc=1, device_id={"tp": peer}, device_id_type=MESH)

    keys = {}
    live = {}

    def remote(key, src, dst, peer):
        i = keys.setdefault(key, len(keys))
        cp = pltpu.make_async_remote_copy(src_ref=src, dst_ref=dst, send_sem=ssem.at[i], recv_sem=rsem.at[i],
                                          device_id={"tp": peer}, device_id_type=MESH)
        cp.start()
        live[key] = cp

    def got(*ks):
        for k in ks:
            live[k].wait_recv()

    g_in = gin_ref[...].astype(F32)
    g_ff = gff_ref[...].astype(F32)

    ri = lax.broadcasted_iota(jnp.int32, (2 * C, 2 * C), 0)
    ci = lax.broadcasted_iota(jnp.int32, (2 * C, 2 * C), 1)
    src_row = jnp.where(ri < C, 2 * ri, 2 * (ri - C) + 1)
    perm = (ci == src_row).astype(BF)
    for blk in range(D // C):
        rows = win_ref[pl.ds(blk * 2 * C, 2 * C), :]
        deint = lax.dot_general(rows, perm, (((0,), (1,)), ((), ())), preferred_element_type=F32).astype(BF)
        wint[0:C, pl.ds(blk * C, C)] = deint[:, 0:C]
        wint[C:2 * C, pl.ds(blk * C, C)] = deint[:, C:2 * C]

    def column(row):
        return jnp.transpose(jnp.broadcast_to(row, (C, C)))

    for j in range(4):
        cols[j] = column(convw_ref[j:j + 1, :].astype(F32))
    cols[4] = column(convb_ref[...].astype(F32))
    cols[5] = column(bdt_ref[...].astype(F32))
    cols[6] = column(dskip_ref[...])

    def small_column(ref):
        w = ref.shape[1]
        eye = lax.broadcasted_iota(jnp.int32, (w, w), 0) == lax.broadcasted_iota(jnp.int32, (w, w), 1)
        v = jnp.where(eye, jnp.broadcast_to(ref[...].astype(F32), (w, w)), 0.0)
        return jnp.broadcast_to(jnp.sum(v, axis=1, keepdims=True), (w, C))

    gp[0:R, :] = small_column(gdt_ref)
    gp[R:R + N, :] = small_column(gb_ref)
    gp[R + N:R + 2 * N, :] = small_column(gc_ref)

    def rms_rows(v, gain):
        return v * lax.rsqrt(jnp.mean(v * v, axis=-1, keepdims=True) + EPSILON) * gain

    def conv_in(_):
        ld_conv.wait()
        for k in range(3):
            for j in range(JB):
                blk = cst[k, pl.ds(j * C, C), :].astype(F32)
                seq[k, j] = jnp.transpose(blk).astype(BF)

    def a_in(_):
        for n in range(N):
            ab[n] = column(-jnp.exp(alogt_ref[n:n + 1, :]) * LOG2E)

    def h_flip():
        def body(n, _):
            for j in range(JB):
                rows = pl.ds(j * C, C)
                hst[n, rows, :] = jnp.transpose(hst[n, rows, :])
            return 0

        lax.fori_loop(0, N, body, 0)

    def h_in(_):
        for cp in ld_h:
            cp.wait()
        h_flip()

    st_state = []

    def state_out(_):
        h_flip()
        for n in range(N):
            st_state.append(local(hst.at[n], ssmo_hbm.at[:, n, :]))
        for k in range(3):
            for j in range(JB):
                cst[k, pl.ds(j * C, C), :] = jnp.transpose(seq[S + k, j].astype(F32)).astype(BF)
        st_state.append(local(cst, convo_hbm))

    def route_prep(s):
        row = ids_ref[s].astype(F32)
        idb = jnp.transpose(jnp.broadcast_to(row, (C, Bt)))
        idsb[s] = idb
        lane = lax.broadcasted_iota(jnp.int32, (Bt, C), 1).astype(F32)
        hot = idb == lane
        before = (lax.broadcasted_iota(jnp.int32, (Bt, Bt), 1) < lax.broadcasted_iota(jnp.int32, (Bt, Bt), 0)).astype(BF)
        cum = jnp.dot(before, hot.astype(BF), preferred_element_type=F32)
        off = jnp.dot(jnp.ones((8, Bt), BF), (idb < lane).astype(BF), preferred_element_type=F32)[0:1, :]
        pos = jnp.sum(jnp.where(hot, cum + off, 0.0), axis=1, keepdims=True)
        posb = jnp.broadcast_to(pos, (Bt, C))
        rcb[...] = idb * float(T) + posb
        pos_row = jnp.transpose(posb)[0:1, :]
        pm[s] = (lax.broadcasted_iota(jnp.int32, (Bt, Bt), 0).astype(F32) == pos_row).astype(BF)
        lane_c = lax.broadcasted_iota(jnp.int32, (Bt, T), 1).astype(F32)

        def body(k, _):
            ubig[s, :, pl.ds(pl.multiple_of(k * T, T), T)] = (rcb[...] == lane_c + k.astype(F32) * T).astype(BF)
            return 0

        lax.fori_loop(0, slots, body, 0)

    def stage_a(s):
        ld_x[s].wait()

        def norm_body(i, _):
            rows = pl.ds(pl.multiple_of(i * 64, 64), 64)
            nbuf[rows, :] = rms_rows(xv[s, rows, :].astype(F32), g_in).astype(BF)
            return 0

        lax.fori_loop(0, Bt // 64, norm_body, 0)
        if s == 0:
            conv_in(0)
        for j in range(JB):
            xz = lax.dot_general(wint[...], nbuf[pl.ds(j * C, C), :], NT, preferred_element_type=F32).astype(BF)
            seq[3 + s, j] = xz[0:C]
            zbuf[s, j] = xz[C:2 * C]
            acc = xz[0:C].astype(F32) * cols[3] + cols[4]
            for k in range(3):
                acc = acc + seq[s + k, j].astype(F32) * cols[k]
            xc = silu(acc).astype(BF)
            xcb[s, j] = xc
            ppk[s, j] = jnp.dot(wxpt_ref[...], xc, preferred_element_type=F32)
        if s == 0:
            pl.semaphore_wait(barrier, 4)
        theirs = pl.ds(pl.multiple_of((1 - c) * PH, PH), PH)
        remote(("p0", s), ppk.at[s, :, theirs], prx.at[s], partner)

    own_half = pl.ds(pl.multiple_of(c * PH, PH), PH)

    def stage_p1(s):
        got(("p0", s))
        ptx[s] = ppk[s, :, own_half, :] + prx[s]
        for k, (peer, j) in enumerate(((right, q_r), (left, q_l), (opp, q_o))):
            remote(("p1", s, k), ptx.at[s, j], prs.at[s, k], peer)

    def stage_p2(s):
        got(*[("p1", s, k) for k in range(3)])
        v = ptx[s, q] + prs[s, 0] + prs[s, 1] + prs[s, 2]
        sq = v * v
        sa = jnp.sum(sq[0:N], axis=0, keepdims=True)
        sb = jnp.sum(sq[N:2 * N], axis=0, keepdims=True)
        whole = (sa + sb) * (1.0 / R)
        first = jnp.where(c == 0, whole, sa * (1.0 / N))
        second = jnp.where(c == 0, whole, sb * (1.0 / N))
        gain = gp[own_half, :]
        pn[s, q, pl.ds(pl.multiple_of(c * PH, PH), N), :] = v[0:N] * lax.rsqrt(first + EPSILON) * gain[0:N]
        pn[s, q, pl.ds(pl.multiple_of(c * PH + N, N), N), :] = v[N:2 * N] * lax.rsqrt(second + EPSILON) * gain[N:2 * N]
        for k, peer in enumerate((right, left, opp)):
            sh = pn.at[s, q, own_half]
            remote(("p2", s, k), sh, sh, peer)

    def stage_p3(s):
        got(*[("p2", s, k) for k in range(3)])
        sh = pn.at[s, :, own_half]
        remote(("p3", s), sh, sh, partner)

    def stage_ssm(s):
        got(("p3", s))
        blk = 64
        for j in range(JB):
            v = lax.dot_general(wdt_ref[...], pn[s, j, 0:R, :].astype(BF), (((0,), (0,)), ((), ())), preferred_element_type=F32) + cols[5]
            dl = jnp.maximum(v, 0.0) + jnp.log1p(jnp.exp(-jnp.abs(v)))
            delta[j] = dl
            dxb[j] = dl * xcb[s, j].astype(F32)

        def body(i, _):
            j = i // (C // blk)
            r0 = (i % (C // blk)) * blk
            rows = pl.ds(pl.multiple_of(r0, blk), blk)
            hrows = pl.ds(pl.multiple_of(j * C + r0, blk), blk)
            d = delta[j, rows, :]
            dx = dxb[j, rows, :]
            acc = cols[6, rows, :] * xcb[s, j, rows, :].astype(F32)
            for n in range(N):
                bb = pn[s, j, R + n:R + n + 1, :]
                cc = pn[s, j, R + N + n:R + N + n + 1, :]
                hn = jnp.exp2(d * ab[n, rows, :]) * hst[n, hrows, :] + dx * bb
                hst[n, hrows, :] = hn
                acc = acc + hn * cc
            ygb[j, rows, :] = (acc * silu(zbuf[s, j, rows, :].astype(F32))).astype(BF)
            return 0

        lax.fori_loop(0, JB * (C // blk), body, 0)
        for j in range(JB):
            y = lax.dot_general(ygb[j], wout_ref[...], (((0,), (0,)), ((), ())), preferred_element_type=F32)
            ypart[s, pl.ds(j * C, C), :] = y.astype(BF)
        rs0("y", s)

    bufs = {"y": (ypart, yrx, ytx1, ytxd, ytx2, yrx1, yrxd, yrx2), "o": (opart, orx, otx1, otxd, otx2, orx1, orxd, orx2)}

    def rs0(w, s):
        part, prx_ = bufs[w][0:2]
        src = pl.ds(pl.multiple_of((1 - c) * half, half), half)
        remote((w, 0, s), part.at[s, src], prx_.at[s], partner)

    def chip_sum(w, s, j, hv):
        part, prx_ = bufs[w][0:2]
        a = part[s, pl.ds(pl.multiple_of(c * half + j * quarter + hv * eighth, eighth), eighth), :].astype(F32)
        b = prx_[s, pl.ds(pl.multiple_of(j * quarter + hv * eighth, eighth), eighth), :].astype(F32)
        return a + b

    def rs1(w, s):
        _, _, tx1, txd, _, rx1, rxd, _ = bufs[w]
        got((w, 0, s))
        tx1[s, 0] = chip_sum(w, s, q_o, 0).astype(BF)
        remote((w, 1, s, 0), tx1.at[s, 0], rx1.at[s, 0], right)
        tx1[s, 1] = chip_sum(w, s, q_o, 1).astype(BF)
        remote((w, 1, s, 1), tx1.at[s, 1], rx1.at[s, 1], left)
        txd[s, 0] = chip_sum(w, s, q_r, 1).astype(BF)
        remote((w, 2, s, 0), txd.at[s, 0], rxd.at[s, 0], right)
        txd[s, 1] = chip_sum(w, s, q_l, 0).astype(BF)
        remote((w, 2, s, 1), txd.at[s, 1], rxd.at[s, 1], left)

    def rs2(w, s):
        _, _, _, _, tx2, rx1, _, rx2 = bufs[w]
        got((w, 1, s, 0))
        tx2[s, 0] = (chip_sum(w, s, q_r, 0) + rx1[s, 0].astype(F32)).astype(BF)
        remote((w, 3, s, 0), tx2.at[s, 0], rx2.at[s, 0], right)
        got((w, 1, s, 1))
        tx2[s, 1] = (chip_sum(w, s, q_l, 1) + rx1[s, 1].astype(F32)).astype(BF)
        remote((w, 3, s, 1), tx2.at[s, 1], rx2.at[s, 1], left)

    def rs3(w, s):
        _, _, _, _, _, _, rxd, rx2 = bufs[w]
        got((w, 2, s, 0), (w, 2, s, 1), (w, 3, s, 0), (w, 3, s, 1))
        lo = chip_sum(w, s, q, 0) + rx2[s, 0].astype(F32) + rxd[s, 1].astype(F32)
        hi = chip_sum(w, s, q, 1) + rx2[s, 1].astype(F32) + rxd[s, 0].astype(F32)
        return lo, hi

    def rows_of(j, hv=None):
        if hv is None:
            return pl.ds(pl.multiple_of(c * half + j * quarter, quarter), quarter)
        return pl.ds(pl.multiple_of(c * half + j * quarter + hv * eighth, eighth), eighth)

    def ag1(w, buf, s):
        own = buf.at[s, rows_of(q)]
        remote((w, 0, s, 0), own, own, right)
        remote((w, 0, s, 1), own, own, left)
        remote((w, 1, s, 0), own, own, partner)

    def ag2(w, buf, s):
        got((w, 0, s, 0))
        fwd = buf.at[s, rows_of(q_l, 0)]
        remote((w, 2, s, 0), fwd, fwd, right)
        got((w, 0, s, 1))
        fwd = buf.at[s, rows_of(q_r, 1)]
        remote((w, 2, s, 1), fwd, fwd, left)
        for k, j in enumerate((q_l, q_r)):
            sh = buf.at[s, rows_of(j)]
            remote((w, 1, s, 1 + k), sh, sh, partner)

    def ag3(w, buf, s):
        got((w, 2, s, 0), (w, 2, s, 1))
        sh = buf.at[s, rows_of(q_o)]
        remote((w, 1, s, 3), sh, sh, partner)

    def ag4(w, s):
        got(*[(w, 1, s, k) for k in range(4)])

    def y3(s):
        sums = rs3("y", s)
        for hv in range(2):
            rows = rows_of(q, hv)
            loc = pl.ds(hv * eighth, eighth)
            u = (xv[s, rows, :].astype(F32) + sums[hv]).astype(BF)
            ubuf[s, loc, :] = u
            mfull[s, rows, :] = rms_rows(u.astype(F32), g_ff).astype(BF)
        ag1("m", mfull, s)
        logits = lax.dot_general(mfull[s, rows_of(q), :], wrt_ref[...], NT, preferred_element_type=F32)
        ex = jnp.exp(logits - jnp.max(logits, axis=-1, keepdims=True))
        ids = idsb[s, rows_of(q), :][:, 0:E]
        pick = jnp.where(lax.broadcasted_iota(jnp.int32, ex.shape, 1).astype(F32) == ids, ex, 0.0)
        prob = jnp.sum(pick, axis=-1, keepdims=True) / jnp.sum(ex, axis=-1, keepdims=True)
        pwb[s] = jnp.broadcast_to(prob, (quarter, C))

    def o3(s):
        sums = rs3("o", s)
        for hv in range(2):
            rows = rows_of(q, hv)
            loc = pl.ds(hv * eighth, eighth)
            pw = pwb[s, loc, :][:, 0:1]
            yfull[s, rows, :] = (ubuf[s, loc, :].astype(F32) + pw * sums[hv]).astype(BF)
        ag1("z", yfull, s)

    group = -(-slots // 4)

    def moe_part(s, part):
        if part == 0:
            msort[...] = jnp.dot(pm[s], mfull[s], preferred_element_type=F32).astype(BF).reshape(tiles, T, D)
        picks = []
        for k in range(part * group, min(slots, (part + 1) * group)):
            tile = tt_ref[s, k]
            picks.append((k, tile, jnp.clip(k - tile, 0, E - 1)))
        for k, tile, e in picks:
            lhs = msort[tile]
            gate = jnp.dot(lhs, wg[e], preferred_element_type=F32)
            up = jnp.dot(lhs, wu[e], preferred_element_type=F32)
            hbuf[k - part * group] = (silu(gate) * up).astype(BF)
        for k, tile, e in picks:
            opair[k * T:(k + 1) * T, :] = jnp.dot(hbuf[k - part * group], wd[e], preferred_element_type=F32).astype(BF)

    def moe_down(s):
        for i in range(Bt // 256):
            rows = pl.ds(i * 256, 256)
            opart[s, rows, :] = jnp.dot(ubig[s, rows, :], opair[...], preferred_element_type=F32).astype(BF)
        rs0("o", s)

    st_y = []

    def y_out(s):
        ag4("z", s)
        st_y.append(local(yfull.at[s], y_hbm.at[s]))

    acts = {
        "A": stage_a, "p1": stage_p1, "p2": stage_p2, "p3": stage_p3, "S": stage_ssm,
        "y1": lambda s: rs1("y", s), "y2": lambda s: rs2("y", s), "y3": y3,
        "m2": lambda s: ag2("m", mfull, s), "m3": lambda s: ag3("m", mfull, s), "m4": lambda s: ag4("m", s),
        "o1": lambda s: rs1("o", s), "o2": lambda s: rs2("o", s), "o3": o3,
        "z2": lambda s: ag2("z", yfull, s), "z3": lambda s: ag3("z", yfull, s), "z4": y_out, "D": moe_down,
        "W": route_prep, "HI": h_in, "AI": a_in, "SO": state_out,
    }
    for k in range(4):
        acts["M%d" % k] = functools.partial(lambda k, s: moe_part(s, k), k)

    def run(*plan):
        for item in plan:
            name, s = item.split(".")
            acts[name](int(s))

    run("A.0", "A.1", "p1.0", "A.2", "p1.1", "A.3", "p1.2", "p2.0", "AI.0", "p1.3", "p2.1", "HI.0", "p3.0", "p2.2", "W.0", "p3.1", "p2.3")
    run("S.0", "p3.2", "S.1", "y1.0", "p3.3", "S.2", "y1.1", "y2.0", "S.3", "y1.2", "y2.1", "y3.0", "W.1")
    run("y1.3", "y2.2", "y3.1", "m2.0", "W.2", "y2.3", "y3.2", "m2.1", "m3.0", "SO.0", "W.3", "m4.0")
    for cp in ld_w:
        cp.wait()
    run("M0.0", "y3.3", "M1.0", "m3.1", "m2.2", "M2.0", "M3.0", "m2.3", "m3.2", "D.0")
    run("m4.1", "M0.1", "m3.3", "M1.1", "o1.0", "M2.1", "M3.1", "o2.0", "D.1")
    run("m4.2", "M0.2", "o3.0", "M1.2", "o1.1", "M2.2", "z2.0", "M3.2", "o2.1", "D.2")
    run("m4.3", "M0.3", "z3.0", "o3.1", "M1.3", "o1.2", "M2.3", "z4.0", "z2.1", "M3.3", "o2.2", "D.3")
    run("z3.1", "o3.2", "o1.3", "z4.1", "z2.2", "o2.3", "z3.2", "o3.3", "z4.2", "z2.3", "z3.3", "z4.3")
    for cp in live.values():
        cp.wait_send()
    for cp in st_state + st_y:
        cp.wait()


def solution(mesh):
    act_spec = P(None, "dp", None)
    state_spec = P("dp", "tp", None)
    in_specs = (act_spec, state_spec, state_spec, act_spec, P(None), P(None, None, "tp"), P("tp", None), P("tp"), P("tp", None), P(None), P(None), P(None), P(None, "tp"), P("tp"), P("tp", None), P("tp"), P("tp", None), P(None), P(None, None), P(None, None, "tp"), P(None, None, "tp"), P(None, "tp", None))
    out_specs = (act_spec, state_spec, state_spec)
    chips = mesh.shape["tp"] // 2
    assert chips == 4

    def layer_steps(x_steps, conv_state, ssm_state, expert_ids, g_in, w_in, conv_w, conv_b, w_xp, g_dt, g_b, g_c, w_dt, b_dt, a_log, d_skip, w_out, g_ff, w_router, w_gate, w_up, w_down):
        S, B, D = x_steps.shape
        C = w_in.shape[2]
        R = w_dt.shape[0]
        N = a_log.shape[1]
        E, _, F = w_gate.shape
        assert expert_ids.shape[2] == 1 and B == 4 * C and R == 2 * N
        T = 128
        tiles = B // T
        slots = E + tiles - 1
        cfg = dict(S=S, B=B, D=D, C=C, N=N, R=R, E=E, F=F, chips=chips, T=T, tiles=tiles, slots=slots)
        k_i = lax.broadcasted_iota(jnp.int32, (S, slots, tiles, B), 1)
        t_i = lax.broadcasted_iota(jnp.int32, (S, slots, tiles, B), 2)
        ids4 = expert_ids.reshape(S, 1, 1, B)
        lo = jnp.sum((ids4 < k_i - t_i).astype(jnp.int32), axis=3)
        hi = jnp.sum((ids4 <= k_i - t_i).astype(jnp.int32), axis=3)
        t3 = lax.broadcasted_iota(jnp.int32, (S, slots, tiles), 2)
        tile_of = jnp.max(jnp.where((hi > lo) & (lo < T * (t3 + 1)) & (hi > T * t3), t3, 0), axis=2)
        row = lambda a: a.reshape(1, a.shape[0])
        vm = pl.BlockSpec(memory_space=pltpu.VMEM)
        anym = pl.BlockSpec(memory_space=pl.ANY)
        half, quarter, eighth = B // 2, B // 8, B // 16
        ring = lambda: [
            pltpu.VMEM((S, B, D), BF), pltpu.VMEM((S, half, D), BF),
            pltpu.VMEM((S, 2, eighth, D), BF), pltpu.VMEM((S, 2, eighth, D), BF), pltpu.VMEM((S, 2, eighth, D), BF),
            pltpu.VMEM((S, 2, eighth, D), BF), pltpu.VMEM((S, 2, eighth, D), BF), pltpu.VMEM((S, 2, eighth, D), BF)]
        n_remote = S * (8 + 2 * 7 + 2 * 8)
        JB = B // C
        scratch = [
            pltpu.VMEM((S, B, D), BF), pltpu.VMEM((3, B, C), BF), pltpu.VMEM((3 + S, JB, C, C), BF), pltpu.VMEM((N, B, C), F32),
            pltpu.VMEM((E, D, F), BF), pltpu.VMEM((E, D, F), BF), pltpu.VMEM((E, F, D), BF),
            pltpu.VMEM((2 * C, D), BF), pltpu.VMEM((N, C, C), F32), pltpu.VMEM((7, C, C), F32), pltpu.VMEM((2 * R, C), F32),
            pltpu.VMEM((B, D), BF), pltpu.VMEM((S, JB, C, C), BF), pltpu.VMEM((S, JB, C, C), BF), pltpu.VMEM((S, B, C), F32),
            pltpu.VMEM((B, C), F32), pltpu.VMEM((S, B, B), BF), pltpu.VMEM((S, B, slots * T), BF), pltpu.VMEM((tiles, T, D), BF),
            pltpu.VMEM((-(-slots // 4), T, F), BF), pltpu.VMEM((slots * T, D), BF),
            pltpu.VMEM((S, JB, 2 * R, C), F32), pltpu.VMEM((S, JB, R, C), F32), pltpu.VMEM((S, JB, R, C), F32),
            pltpu.VMEM((S, 3, R, C), F32), pltpu.VMEM((S, JB, 2 * R, C), F32),
            pltpu.VMEM((JB, C, C), F32), pltpu.VMEM((JB, C, C), F32), pltpu.VMEM((JB, C, C), BF),
            *ring(), *ring(),
            pltpu.VMEM((S, quarter, D), BF), pltpu.VMEM((S, quarter, C), F32),
            pltpu.VMEM((S, B, D), BF), pltpu.VMEM((S, B, D), BF),
            pltpu.SemaphoreType.DMA((2 * S + 2 + 2 * N + 3,)),
            pltpu.SemaphoreType.DMA((n_remote,)), pltpu.SemaphoreType.DMA((n_remote,)),
        ]
        y, conv_o, ssm_o = pl.pallas_call(
            functools.partial(layer_kernel, cfg),
            out_shape=(jax.ShapeDtypeStruct((S, B, D), BF), jax.ShapeDtypeStruct((3, B, C), BF), jax.ShapeDtypeStruct((B, N, C), F32)),
            in_specs=[anym] * 3 + [pl.BlockSpec(memory_space=pltpu.SMEM)] + [vm] * 16 + [anym] * 3,
            out_specs=(anym, anym, anym),
            scratch_shapes=scratch,
            compiler_params=pltpu.CompilerParams(collective_id=0, has_side_effects=True, vmem_limit_bytes=62 * 1024 * 1024),
            name="layer_steps",
        )(x_steps, conv_state.transpose(2, 0, 1), ssm_state.transpose(0, 2, 1), tile_of, expert_ids.transpose(0, 2, 1), row(g_in), row(g_ff),
          row(g_dt), row(g_b), row(g_c), w_in.reshape(2 * D, C), conv_w.T, row(conv_b), w_xp.T, w_dt, row(b_dt), a_log.T, row(d_skip),
          w_out, w_router.T, w_gate, w_up, w_down)
        return y, conv_o.transpose(1, 2, 0), ssm_o.transpose(0, 2, 1)

    return jax.shard_map(layer_steps, mesh=mesh, in_specs=in_specs, out_specs=out_specs, check_vma=False)
```

time: 145 us -> 111 us (0.77)
  the two profiles are of different devices: /device:TPU:80 before, /device:TPU:123 now
where the time goes in v2:
time: 111 us
  Pallas kernels  96.3 us (87%)
  local copies, waits for them, and re-layouts  10.2 us (9%)
  other arithmetic  3.38 us (3%)
    pallas_call x1, Pallas kernels, layer_steps(): pl.pallas_call(functools.partial(layer_kernel, cfg), out_shape=(jax.Shape...  96.3 us
    unnamed x6, local copies, waits for them, and re-layouts  7.69 us
    reduce_sum x1, other arithmetic, layer_steps(): lo = jnp.sum((ids4 < k_i - t_i).astype(jnp.int32), axis=3)  2.65 us
    reshape x2, local copies, waits for them, and re-layouts, layer_steps(): row = lambda a: a.reshape(1, a.shape[0])  2.52 us

profile of v2, /device:TPU:123, one launch (start us, length us, event | category | flops | bytes accessed | tf_op | source)
XLA Modules:
  0.0 110.5 jit_solution(2022716005056964035)
XLA Ops:
  0.6 1.3 %reshape.35.gin_ref = bf16[1,512]{1,0:T(2,128)(2,1)} reshape(bf16[512]{0:T(512)(128)(2,1)} %param.26) | data formatting | bytes 2048 | tf_op jit(solution)/shard_map/reshape | solution.py:437
  1.9 1.3 %reshape.36.gff_ref = bf16[1,512]{1,0:T(2,128)(2,1)} reshape(bf16[512]{0:T(512)(128)(2,1)} %param.39) | data formatting | bytes 2048 | tf_op jit(solution)/shard_map/reshape | solution.py:437
  3.2 0.7 copy.29
  3.9 2.6 %convert_reduce_fusion = (s32[4,19,4]{2,1,0:T(8,128)S(1)}, s32[4,19,4]{2,1,0:T(8,128)S(1)}) fusion(s32[4,512]{1,0:T(4,128)S(1)} %bitcast.25), kind=kLoop, calls=%fused_computation | loop fusion | flops 1088928 | bytes 10624 | tf_op jit(solution)/shard_map/reduce_sum | solution.py:433
  6.5 0.7 select_reduce_fusion.tt_ref
  7.2 96.3 %layer_steps.1 = (bf16[4,512,512]{2,1,0:T(8,128)(2,1)}, bf16[3,512,128]{2,1,0:T(8,128)(2,1)}, f32[512,16,128]{2,1,0:T(8,128)}) custom-call(bf16[4,512,512]{2,1,0:T(8,128)(2,1)} %x_hbm.1, bf16[3,512,128]{2,1,0:T(8,128)(2,1)} %bitcast.22, f32[512,16,128]{2,1,0:T(8,128)} %bitcast.19, s32[4,19]{1,0:T(4,128)} %select_reduce_fusion.tt_ref, s32[4,1,512]{2,1,0:T(1,128)} %bitcast.24, ...), custom_call_target="tpu_custom_call" | custom-call | tf_op jit(solution)/shard_map/layer_steps/pallas_call | solution.py:463
  103.5 0.0 copy-start
  103.6 3.2 %copy.33 = bf16[4,512,512]{2,1,0:T(8,128)(2,1)} copy(bf16[4,512,512]{2,1,0:T(8,128)(2,1)} %get-tuple-element.16) | data formatting | bytes 4194304
  106.8 1.8 %copy.34 = bf16[512,128,3]{1,0,2:T(8,128)(2,1)} copy(bf16[512,128,3]{1,0,2:T(8,128)(2,1)} %bitcast.21) | data formatting | bytes 786432
  108.5 0.0 copy-done
  108.5 2.0 %copy.35 = f32[512,128,16]{1,2,0:T(8,128)} copy(f32[512,128,16]{1,2,0:T(8,128)S(1)} %bitcast.20) | data formatting | bytes 8388608
  (1 shorter events, 0.0 us)
Async XLA Ops:
  103.5 5.0 %copy-start = (f32[512,16,128]{2,1,0:T(8,128)S(1)}, f32[512,16,128]{2,1,0:T(8,128)}, u32[]{:S(2)}) copy-start(f32[512,16,128]{2,1,0:T(8,128)} %get-tuple-element.8) | copy-start | bytes 12582916
